TPU v7x, 32 devices: a whole 2x2x4 slice. The times are simulated.
32 devices in a mesh: row: 4 (over y, x), col: 4 (over z), depth: 2 (over core).
Axes of the slice: x: 2, y: 2, z: 4, core: 2. Of those that a mesh axis runs over, the one named last changes fastest.
Arguments:
- orbitals: bfloat16 [2, 1024, 2, 4096], P(None, ('row', 'col'), 'depth'), may hold values from -20 to 20
- potential: float32 [2, 4096], P('depth'), may hold values from -6 to 6
Outputs:
- intersection: float32 [1024, 2, 1024], P(('row', 'depth'), None, 'col')
- applied: bfloat16 [2, 1024, 2, 4096], P(None, ('row', 'col'), 'depth')
All inputs are finite; a program needn't handle non-finite values.
Results may differ from a plain program's by a relative error of at most 0.001.
Values may be sent and summed in bfloat16 or wider, within the bound.
A program may use at most 128 MiB of HBM per device.

v0:
```python
import jax
import jax.numpy as jnp
from jax import lax
from jax.sharding import PartitionSpec as P

NX = 64


def with_halo(block, sides, width):
    for axis, dim in sides:
        count = lax.axis_size(axis)
        forward = [(i, i + 1) for i in range(count - 1)]
        forward.append((count - 1, 0))
        backward = [(target, source) for source, target in forward]
        low = lax.ppermute(
            lax.slice_in_dim(block, block.shape[dim] - width, None, axis=dim), axis, forward
        )
        high = lax.ppermute(lax.slice_in_dim(block, 0, width, axis=dim), axis, backward)
        block = jnp.concatenate([low, block, high], axis=dim)
    return block


def apply_operator(padded, potential):
    center = padded[:, :, 1:-1].astype(jnp.float32)
    below = padded[:, :, :-2].astype(jnp.float32)
    above = padded[:, :, 2:].astype(jnp.float32)
    flat_cells = center.shape[-1]
    xpos = jnp.arange(flat_cells) % NX
    yminus = jnp.roll(center, NX, axis=3)
    yplus = jnp.roll(center, -NX, axis=3)
    xminus = jnp.where(xpos == 0, jnp.roll(center, 1 - NX, axis=3), jnp.roll(center, 1, axis=3))
    xplus = jnp.where(
        xpos == NX - 1, jnp.roll(center, NX - 1, axis=3), jnp.roll(center, -1, axis=3)
    )
    lap = below + above + yminus + yplus + xminus + xplus - 6.0 * center
    return (-0.5 * lap + potential[None, None] * center).astype(jnp.bfloat16)


def contract(left, right):
    return lax.dot_general(
        left, right, (((1,), (1,)), ((), ())), preferred_element_type=jnp.float32
    )


def shards(orbitals, potential):
    parts, orbs, planes, cells = orbitals.shape
    flat = orbitals.reshape(parts, orbs, planes * cells)
    panel = lax.all_gather(flat, "col", axis=1, tiled=True)
    other = lax.all_gather(flat, "row", axis=1, tiled=True)
    padded = with_halo(orbitals, (("depth", 2),), 1)
    applied = apply_operator(padded, potential)
    dvol = 1.0 / (planes * lax.axis_size("depth") * cells)
    tile_cols = other.shape[1]
    real_rows = panel[0]
    imag_rows = panel[1]
    sreal = contract(real_rows, other[0]) + contract(imag_rows, other[1])
    simag = contract(real_rows, other[1]) - contract(imag_rows, other[0])
    summed = lax.psum_scatter(
        dvol * jnp.concatenate([sreal, simag], axis=1), "depth", scatter_dimension=0, tiled=True
    )
    intersection = summed.reshape(summed.shape[0], 2, tile_cols)
    intersection = lax.all_to_all(intersection, "col", split_axis=2, concat_axis=2, tiled=True)
    return (intersection, applied)


def solution(mesh):
    in_specs = (P(None, ("row", "col"), "depth", None), P("depth", None))
    out_specs = (P(("row", "depth"), None, "col"), P(None, ("row", "col"), "depth", None))
    return jax.shard_map(shards, mesh=mesh, in_specs=in_specs, out_specs=out_specs, check_vma=False)
```

profile of v0, /device:TPU:0, one launch (start us, length us, event | category | flops | bytes accessed | tf_op | source)
XLA Modules:
  0.0 186.1 jit_solution(16060242905263434024)
XLA Ops:
  7.2 0.0 all-gather.7.cloned.1.call-start
  7.2 0.7 all-gather.7.cloned.1.call-update
  7.9 0.0 all-gather.5.cloned.1.call-start
  8.0 0.7 all-gather.5.cloned.1.call-update
  8.7 0.0 reduce-scatter.2.cloned.1.call-start
  8.7 0.6 collective-permute-start
  9.3 0.1 collective-permute-start.1
  9.4 0.1 fusion.23
  9.4 0.7 fusion.20
  10.1 0.7 fusion.19
  10.8 1.8 fusion.21
  12.7 2.4 %fusion.22 = (f32[2,64,1,4032]{3,1,2,0:T(8,128)}, f32[2,64,1,4032]{3,1,2,0:T(8,128)}) fusion(bf16[2,64,1,4096]{3,1,2,0:T(8,128)(2,1)S(1)} %copy-done), kind=kLoop, calls=%fused_computation.32 | loop fusion | bytes 8257536 | tf_op jit(solution)/shard_map/jit(_roll_static)/slice | solution.py:30
  15.1 50.1 %all-gather.7.cloned.1.call-done = bf16[2,256,1,4096]{3,1,2,0:T(8,128)(2,1)} async-done(((bf16[2,64,1,4096]{3,1,2,0:T(8,128)(2,1)}), bf16[2,256,1,4096]{3,1,2,0:T(8,128)(2,1)}) %all-gather.7.cloned.1.call-update) | async-done | bytes 4194320 | tf_op jit(solution)/shard_map/all_gather | solution.py:49
  65.2 82.3 %all-gather.5.cloned.1.call-done = bf16[2,256,1,4096]{3,1,2,0:T(8,128)(2,1)} async-done(((bf16[2,64,1,4096]{3,1,2,0:T(8,128)(2,1)}), bf16[2,256,1,4096]{3,1,2,0:T(8,128)(2,1)}) %all-gather.5.cloned.1.call-update) | async-done | bytes 4194320 | tf_op jit(solution)/shard_map/all_gather | solution.py:48
  147.5 3.1 %fusion.7 = f32[256,256]{0,1:T(8,128)S(1)} fusion(bf16[2,256,1,4096]{3,1,2,0:T(8,128)(2,1)} %all-gather.5.cloned.1.call-done, bf16[2,256,1,4096]{3,1,2,0:T(8,128)(2,1)} %all-gather.7.cloned.1.call-done), kind=kOutput, calls=%fused_computation.14 | convolution fusion | flops 536870912 | bytes 4456448 | tf_op jit(solution)/shard_map/dot_general | solution.py:40
  150.6 0.3 copy-done.2
  150.9 2.5 %fusion.8 = f32[256,256]{0,1:T(8,128)S(1)} fusion(bf16[2,256,1,4096]{3,1,2,0:T(8,128)(2,1)} %all-gather.5.cloned.1.call-done, bf16[2,256,1,4096]{3,1,2,0:T(8,128)(2,1)S(1)} %copy-done.2), kind=kOutput, calls=%fused_computation.15 | convolution fusion | flops 536870912 | bytes 4456448 | tf_op jit(solution)/shard_map/dot_general | solution.py:40
  153.4 0.3 copy-done.3
  153.8 0.7 fusion.12
  154.5 0.7 fusion.11
  155.3 0.8 maximum_multiply_fusion
  156.1 0.0 reduce-scatter.2.cloned.1.call-update
  156.1 0.6 fusion.15
  156.7 2.4 %fusion.18 = (f32[2,64,1,4095]{3,1,2,0:T(8,128)}, f32[2,64,1,4095]{3,1,2,0:T(8,128)}) fusion(bf16[2,64,1,4096]{3,1,2,0:T(8,128)(2,1)S(1)} %copy-done), kind=kLoop, calls=%fused_computation.28 | loop fusion | bytes 8386560 | tf_op jit(solution)/shard_map/jit(_roll_static)/slice | solution.py:33
  159.1 3.5 %reduce-scatter.2.cloned.1.call-done = f32[128,512]{0,1:T(8,128)} async-done(((f32[256,512]{0,1:T(8,128)}), f32[128,512]{0,1:T(8,128)}) %reduce-scatter.2.cloned.1.call-update) | async-done | bytes 262160 | tf_op jit(solution)/shard_map/reduce_scatter | solution.py:58
  162.7 1.9 copy.7
  164.5 4.8 %all-to-all-start = ((f32[128,2,256]{0,1,2:T(2,128)}), f32[128,2,256]{0,1,2:T(2,128)S(1)}, u32[]{:S(2)}, u32[]{:S(2)}) async-start(f32[128,2,256]{0,1,2:T(2,128)} %copy.7), calls=%async_computation.1 | async-start | bytes 524288 | tf_op jit(solution)/shard_map/all_to_all | solution.py:62
  169.3 0.0 collective-permute-done
  169.3 0.0 collective-permute-done.1
  169.3 6.8 %fusion.6 = bf16[2,64,1,4096]{3,1,2,0:T(8,128)(2,1)} fusion(f32[2,64,1,4032]{3,1,2,0:T(8,128)} %get-tuple-element.15, f32[2,64,1,64]{3,1,2,0:T(8,128)S(1)} %get-tuple-element.17, f32[2,64,1,64]{3,1,2,0:T(8,128)S(1)} %get-tuple-element.16, f32[2,64,1,4032]{3,1,2,0:T(8,128)} %get-tuple-element.14, f32[2,64,1,63]{3,1,2,0:T(8,128)} %get-tuple-element.11, ...), kind=kLoop, calls=%fused_computation.11 | loop fusion | flops 11534336 | bytes 16801792 | tf_op jit(solution)/shard_map/convert_element_type | solution.py:36
  176.2 2.6 %all-to-all-done = f32[128,2,256]{0,1,2:T(2,128)S(1)} async-done(((f32[128,2,256]{0,1,2:T(2,128)}), f32[128,2,256]{0,1,2:T(2,128)S(1)}, u32[]{:S(2)}, u32[]{:S(2)}) %all-to-all-start) | async-done | bytes 262176 | tf_op jit(solution)/shard_map/all_to_all | solution.py:62
  178.7 0.8 copy.8
  (6 shorter events, 0.0 us)
Async XLA Ops:
  7.2 1.5 copy-start
  7.2 58.0 %all-gather.7.cloned.1.call-start = ((), (), s32[]{:S(2)}) async-start(), calls=%async_computation.4 | async-start | bytes 5242880 | tf_op jit(solution)/shard_map/all_gather | solution.py:49
  7.9 139.6 %all-gather.5.cloned.1.call-start = ((), (), s32[]{:S(2)}) async-start(), calls=%async_computation.3 | async-start | bytes 5242880 | tf_op jit(solution)/shard_map/all_gather | solution.py:48
  8.7 154.0 %reduce-scatter.2.cloned.1.call-start = ((), (), s32[]{:S(2)}) async-start(), calls=%async_computation.2 | async-start | bytes 786432 | tf_op jit(solution)/shard_map/reduce_scatter | solution.py:58
  8.7 160.6 %collective-permute-start = (bf16[2,64,1,4096]{3,1,2,0:T(8,128)(2,1)S(1)}, bf16[2,64,1,4096]{3,1,2,0:T(8,128)(2,1)}, u32[]{:S(2)}, u32[]{:S(2)}) collective-permute-start(bf16[2,64,1,4096]{3,1,2,0:T(8,128)(2,1)S(1)} %copy-done), channel_id=1, source_target_pairs={{0,1},{1,0},{2,3},{3,2},{4,5},{5,4},{6,7},{7,6},{8,9},{9,8},{10,11... | collective-permute-start | bytes 3145736 | tf_op jit(solution)/shard_map/ppermute | solution.py:15
  9.3 160.1 %collective-permute-start.1 = (bf16[2,64,1,4096]{3,1,2,0:T(8,128)(2,1)S(1)}, bf16[2,64,1,4096]{3,1,2,0:T(8,128)(2,1)}, u32[]{:S(2)}, u32[]{:S(2)}) collective-permute-start(bf16[2,64,1,4096]{3,1,2,0:T(8,128)(2,1)S(1)} %copy-done), channel_id=1, source_target_pairs={{1,0},{0,1},{3,2},{2,3},{5,4},{4,5},{7,6},{6,7},{9,8},{8,9},{11,10... | collective-permute-start | bytes 3145736 | tf_op jit(solution)/shard_map/ppermute | solution.py:18
  147.5 3.4 %copy-start.2 = (bf16[2,256,1,4096]{3,1,2,0:T(8,128)(2,1)S(1)}, bf16[2,256,1,4096]{3,1,2,0:T(8,128)(2,1)}, u32[]{:S(2)}) copy-start(bf16[2,256,1,4096]{3,1,2,0:T(8,128)(2,1)} %all-gather.7.cloned.1.call-done) | copy-start | bytes 12582916
  150.9 2.8 %copy-start.3 = (bf16[2,256,1,4096]{3,1,2,0:T(8,128)(2,1)S(1)}, bf16[2,256,1,4096]{3,1,2,0:T(8,128)(2,1)}, u32[]{:S(2)}) copy-start(bf16[2,256,1,4096]{3,1,2,0:T(8,128)(2,1)} %all-gather.5.cloned.1.call-done) | copy-start | bytes 12582916
  156.7 12.6 %copy-start.1 = (f32[1,4096]{1,0:T(1,128)S(1)}, f32[1,4096]{1,0:T(1,128)}, u32[]{:S(2)}) copy-start(f32[1,4096]{1,0:T(1,128)} %param.3) | copy-start | bytes 49156
  164.5 14.2 %all-to-all-start = ((f32[128,2,256]{0,1,2:T(2,128)}), f32[128,2,256]{0,1,2:T(2,128)S(1)}, u32[]{:S(2)}, u32[]{:S(2)}) async-start(f32[128,2,256]{0,1,2:T(2,128)} %copy.7), calls=%async_computation.1 | async-start | bytes 524288 | tf_op jit(solution)/shard_map/all_to_all | solution.py:62
Sparse Core Ops, SparseCore 0:
  9.8 55.2 all-gather.6
  66.7 80.7 all-gather.4
  156.2 6.3 reduce-scatter.1
where the time goes:
time: 186 us
  waiting for transfers between devices  140 us (75%)
  between operations  13.8 us (7%)
  local copies, waits for them, and re-layouts  11.5 us (6%)
  other arithmetic  8.25 us (4%)
  matrix products  7.07 us (4%)
  starting transfers between devices  5.54 us (3%)
    all_gather x1, waiting for transfers between devices, shards(): panel = lax.all_gather(flat, 'col', axis=1, tiled=True)  82.3 us
    all_gather x1, waiting for transfers between devices, shards(): other = lax.all_gather(flat, 'row', axis=1, tiled=True)  50.1 us
    dot_general x4, matrix products, contract(): lax.dot_general(left, right, (((1,), (1,)), ((), ())), preferred_element_...  7.07 us
    convert_element_type x1, other arithmetic, apply_operator(): return (-0.5 * lap + potential[None, None] * center).astype(jnp.bfloat16)  6.81 us
    all_to_all x1, starting transfers between devices, shards(): lax.all_to_all(intersection, 'col', split_axis=2, concat_axis=2, tiled=True)  4.79 us
  transfers between devices with their start and end apart: 6, of which 4 were waited for; matrix products, arithmetic and copies ran while one was open for 14% of the time, Pallas kernels for 0%

commit v1 on v0

--- a/solution.py
+++ b/solution.py
@@ -45,7 +45,10 @@
 def shards(orbitals, potential):
     parts, orbs, planes, cells = orbitals.shape
     flat = orbitals.reshape(parts, orbs, planes * cells)
-    panel = lax.all_gather(flat, "col", axis=1, tiled=True)
+    size = lax.axis_size("col")
+    shards_2 = jnp.stack([flat for _ in range(size)])
+    shards_2 = lax.all_to_all(shards_2, "col", split_axis=0, concat_axis=0)
+    panel = jnp.concatenate(shards_2, axis=1)
     other = lax.all_gather(flat, "row", axis=1, tiled=True)
     padded = with_halo(orbitals, (("depth", 2),), 1)
     applied = apply_operator(padded, potential)

time: 186 us -> 156 us (0.84)
  waiting for transfers between devices: 140 us -> 93.8 us
  local copies, waits for them, and re-layouts: 11.5 us -> 20.3 us
  starting transfers between devices: 5.54 us -> 11.9 us
    all_to_all x0 -> x1, waiting for transfers between devices: none -> 86.3 us  [shards(): shards_2 = lax.all_to_all(shards_2, 'col', split_axis=0, concat_axis=0)]
    all_gather x1 -> x0, waiting for transfers between devices: 82.3 us -> none  [shards(): panel = lax.all_gather(flat, 'col', axis=1, tiled=True)]
    all_gather x1, waiting for transfers between devices: 50.1 us -> 0.01 us  [shards(): other = lax.all_gather(flat, 'row', axis=1, tiled=True)]
    all_to_all x0 -> x1, starting transfers between devices: none -> 6.48 us  [shards(): shards_2 = lax.all_to_all(shards_2, 'col', split_axis=0, concat_axis=0)]
    slice x0 -> x1, local copies, waits for them, and re-layouts: none -> 4.75 us  [shards(): real_rows = panel[0]]
    another operation x0 -> x1, local copies, waits for them, and re-layouts: none -> 3.71 us  [shards(): shards_2 = jnp.stack([flat for _ in range(size)])]
  transfers between devices with their start and end apart: 6 -> 6, of which waited for: 4 -> 3; matrix products, arithmetic and copies ran while one was open for 14% -> 19% of each run, Pallas kernels for 0% -> 0%
where the time goes in v1:
time: 156 us
  waiting for transfers between devices  93.8 us (60%)
  local copies, waits for them, and re-layouts  20.3 us (13%)
  between operations  14.1 us (9%)
  starting transfers between devices  11.9 us (8%)
  other arithmetic  8.26 us (5%)
  matrix products  7.28 us (5%)
    all_to_all x1, waiting for transfers between devices, shards(): shards_2 = lax.all_to_all(shards_2, 'col', split_axis=0, concat_axis=0)  86.3 us
    dot_general x4, matrix products, contract(): lax.dot_general(left, right, (((1,), (1,)), ((), ())), preferred_element_...  7.28 us
    convert_element_type x1, other arithmetic, apply_operator(): return (-0.5 * lap + potential[None, None] * center).astype(jnp.bfloat16)  6.81 us
    all_to_all x1, starting transfers between devices, shards(): shards_2 = lax.all_to_all(shards_2, 'col', split_axis=0, concat_axis=0)  6.48 us
    all_to_all x1, starting transfers between devices, shards(): lax.all_to_all(intersection, 'col', split_axis=2, concat_axis=2, tiled=True)  4.82 us
    slice x1, local copies, waits for them, and re-layouts, shards(): real_rows = panel[0]  4.75 us
    reduce_scatter x1, waiting for transfers between devices, shards(): lax.psum_scatter(dvol * jnp.concatenate([sreal, simag], axis=1), 'depth',...  4.2 us
    another operation x1, local copies, waits for them, and re-layouts, shards(): shards_2 = jnp.stack([flat for _ in range(size)])  3.71 us
  transfers between devices with their start and end apart: 6, of which 3 were waited for; matrix products, arithmetic and copies ran while one was open for 19% of the time, Pallas kernels for 0%

profile of v1, /device:TPU:0, one launch (start us, length us, event | category | flops | bytes accessed | tf_op | source)
XLA Modules:
  0.0 155.6 jit_solution(7314318121682118000)
XLA Ops:
  7.2 3.7 %stack.3 = bf16[4,2,64,4096]{3,2,1,0:T(8,128)(2,1)} broadcast(bf16[2,64,4096]{2,1,0:T(8,128)(2,1)} %bitcast.22), dimensions={1,2,3} | broadcast | bytes 5242880 | tf_op jit(solution)/shard_map/stack | solution.py:49
  10.9 6.5 %all-to-all-start = ((bf16[4,2,64,4096]{3,2,1,0:T(8,128)(2,1)}), bf16[4,2,64,4096]{3,2,1,0:T(8,128)(2,1)}, u32[]{:S(2)}, u32[]{:S(2)}) async-start(bf16[4,2,64,4096]{3,2,1,0:T(8,128)(2,1)} %stack.3), calls=%async_computation | async-start | bytes 8388608 | tf_op jit(solution)/shard_map/all_to_all | solution.py:50
  17.4 0.0 all-gather.3.cloned.1.call-start
  17.4 0.7 all-gather.3.cloned.1.call-update
  18.1 0.0 reduce-scatter.2.cloned.1.call-start
  18.1 0.1 collective-permute-start
  18.2 0.5 collective-permute-start.1
  18.7 0.1 fusion.24
  18.8 0.7 fusion.21
  19.5 0.7 fusion.20
  20.2 1.8 %fusion.22 = (f32[2,64,1,4033]{3,1,2,0:T(8,128)S(1)}, f32[2,64,1,4033]{3,1,2,0:T(8,128)}) fusion(bf16[2,64,1,4096]{3,1,2,0:T(8,128)(2,1)S(1)} %copy-done), kind=kLoop, calls=%fused_computation.30 | loop fusion | bytes 8259584 | tf_op jit(solution)/shard_map/jit(_roll_static)/slice | solution.py:33
  22.0 2.4 %fusion.23 = (f32[2,64,1,4032]{3,1,2,0:T(8,128)}, f32[2,64,1,4032]{3,1,2,0:T(8,128)}) fusion(bf16[2,64,1,4096]{3,1,2,0:T(8,128)(2,1)S(1)} %copy-done), kind=kLoop, calls=%fused_computation.31 | loop fusion | bytes 8257536 | tf_op jit(solution)/shard_map/jit(_roll_static)/slice | solution.py:30
  24.4 86.3 %all-to-all-done = bf16[4,2,64,4096]{3,2,1,0:T(8,128)(2,1)} async-done(((bf16[4,2,64,4096]{3,2,1,0:T(8,128)(2,1)}), bf16[4,2,64,4096]{3,2,1,0:T(8,128)(2,1)}, u32[]{:S(2)}, u32[]{:S(2)}) %all-to-all-start) | async-done | bytes 4194336 | tf_op jit(solution)/shard_map/all_to_all | solution.py:50
  110.8 4.8 %fusion.18 = (bf16[1,4,64,4096]{3,2,0,1:T(8,128)(2,1)}, bf16[1,4,64,4096]{3,2,0,1:T(8,128)(2,1)}) fusion(bf16[2,4,64,4096]{3,2,0,1:T(8,128)(2,1)} %bitcast.1), kind=kLoop, calls=%fused_computation.26 | loop fusion | bytes 8388608 | tf_op jit(solution)/shard_map/slice | solution.py:57
  115.5 3.1 %fusion.7 = f32[256,256]{0,1:T(8,128)S(1)} fusion(bf16[256,4096]{1,0:T(8,128)(2,1)} %bitcast.23, bf16[2,256,1,4096]{3,1,2,0:T(8,128)(2,1)} %all-gather.3.cloned.1.call-done), kind=kOutput, calls=%fused_computation.12 | convolution fusion | flops 536870912 | bytes 4456448 | tf_op jit(solution)/shard_map/dot_general | solution.py:40
  118.7 2.7 %fusion.8 = f32[256,256]{0,1:T(8,128)S(1)} fusion(bf16[256,4096]{1,0:T(8,128)(2,1)S(1)} %bitcast.25, bf16[2,256,1,4096]{3,1,2,0:T(8,128)(2,1)} %all-gather.3.cloned.1.call-done), kind=kOutput, calls=%fused_computation.13 | convolution fusion | flops 536870912 | bytes 4456448 | tf_op jit(solution)/shard_map/dot_general | solution.py:40
  121.4 0.1 copy-done.4
  121.5 0.7 fusion.12
  122.2 0.8 copy-done.1
  123.1 0.7 fusion.11
  123.8 0.8 maximum_multiply_fusion
  124.6 0.0 reduce-scatter.2.cloned.1.call-update
  124.7 0.6 fusion.15
  125.3 2.4 %fusion.19 = (f32[2,64,1,4095]{3,1,2,0:T(8,128)}, f32[2,64,1,4095]{3,1,2,0:T(8,128)}) fusion(bf16[2,64,1,4096]{3,1,2,0:T(8,128)(2,1)S(1)} %copy-done), kind=kLoop, calls=%fused_computation.27 | loop fusion | bytes 8386560 | tf_op jit(solution)/shard_map/jit(_roll_static)/slice | solution.py:33
  127.7 4.2 %reduce-scatter.2.cloned.1.call-done = f32[128,512]{0,1:T(8,128)} async-done(((f32[256,512]{0,1:T(8,128)}), f32[128,512]{0,1:T(8,128)}) %reduce-scatter.2.cloned.1.call-update) | async-done | bytes 262160 | tf_op jit(solution)/shard_map/reduce_scatter | solution.py:61
  131.9 1.9 %copy.7 = f32[128,2,256]{0,1,2:T(2,128)} copy(f32[128,2,256]{0,2,1:T(8,128)} %bitcast.27) | data formatting | bytes 524288 | tf_op jit(solution)/shard_map/reshape | solution.py:64
  133.8 4.8 %all-to-all-start.1 = ((f32[128,2,256]{0,1,2:T(2,128)}), f32[128,2,256]{0,1,2:T(2,128)S(1)}, u32[]{:S(2)}, u32[]{:S(2)}) async-start(f32[128,2,256]{0,1,2:T(2,128)} %copy.7), calls=%async_computation.2 | async-start | bytes 524288 | tf_op jit(solution)/shard_map/all_to_all | solution.py:65
  138.6 0.0 collective-permute-done
  138.6 0.0 collective-permute-done.1
  138.6 6.8 %fusion.6 = bf16[2,64,1,4096]{3,1,2,0:T(8,128)(2,1)} fusion(f32[2,64,1,4032]{3,1,2,0:T(8,128)} %get-tuple-element.17, f32[2,64,1,64]{3,1,2,0:T(8,128)S(1)} %get-tuple-element.19, f32[2,64,1,64]{3,1,2,0:T(8,128)S(1)} %get-tuple-element.18, f32[2,64,1,4032]{3,1,2,0:T(8,128)} %get-tuple-element.16, f32[2,64,1,63]{3,1,2,0:T(8,128)} %get-tuple-element.13, ...), kind=kLoop, calls=%fused_computation.9 | loop fusion | flops 11534336 | bytes 16801792 | tf_op jit(solution)/shard_map/convert_element_type | solution.py:36
  145.4 2.5 %all-to-all-done.1 = f32[128,2,256]{0,1,2:T(2,128)S(1)} async-done(((f32[128,2,256]{0,1,2:T(2,128)}), f32[128,2,256]{0,1,2:T(2,128)S(1)}, u32[]{:S(2)}, u32[]{:S(2)}) %all-to-all-start.1) | async-done | bytes 262176 | tf_op jit(solution)/shard_map/all_to_all | solution.py:65
  148.0 0.8 copy.8
  (9 shorter events, 0.0 us)
Async XLA Ops:
  10.9 7.3 %copy-start = (bf16[2,64,1,4096]{3,1,2,0:T(8,128)(2,1)S(1)}, bf16[2,64,1,4096]{3,1,2,0:T(8,128)(2,1)}, u32[]{:S(2)}) copy-start(bf16[2,64,1,4096]{3,1,2,0:T(8,128)(2,1)} %param.2) | copy-start | bytes 3145732
  10.9 99.9 %all-to-all-start = ((bf16[4,2,64,4096]{3,2,1,0:T(8,128)(2,1)}), bf16[4,2,64,4096]{3,2,1,0:T(8,128)(2,1)}, u32[]{:S(2)}, u32[]{:S(2)}) async-start(bf16[4,2,64,4096]{3,2,1,0:T(8,128)(2,1)} %stack.3), calls=%async_computation | async-start | bytes 8388608 | tf_op jit(solution)/shard_map/all_to_all | solution.py:50
  17.4 98.2 %all-gather.3.cloned.1.call-start = ((), (), s32[]{:S(2)}) async-start(), calls=%async_computation.4 | async-start | bytes 5242880 | tf_op jit(solution)/shard_map/all_gather | solution.py:52
  18.1 113.8 %reduce-scatter.2.cloned.1.call-start = ((), (), s32[]{:S(2)}) async-start(), calls=%async_computation.3 | async-start | bytes 786432 | tf_op jit(solution)/shard_map/reduce_scatter | solution.py:61
  18.1 120.5 %collective-permute-start = (bf16[2,64,1,4096]{3,1,2,0:T(8,128)(2,1)S(1)}, bf16[2,64,1,4096]{3,1,2,0:T(8,128)(2,1)}, u32[]{:S(2)}, u32[]{:S(2)}) collective-permute-start(bf16[2,64,1,4096]{3,1,2,0:T(8,128)(2,1)S(1)} %copy-done), channel_id=1, source_target_pairs={{0,1},{1,0},{2,3},{3,2},{4,5},{5,4},{6,7},{7,6},{8,9},{9,8},{10,11... | collective-permute-start | bytes 3145736 | tf_op jit(solution)/shard_map/ppermute | solution.py:15
  18.2 120.4 %collective-permute-start.1 = (bf16[2,64,1,4096]{3,1,2,0:T(8,128)(2,1)S(1)}, bf16[2,64,1,4096]{3,1,2,0:T(8,128)(2,1)}, u32[]{:S(2)}, u32[]{:S(2)}) collective-permute-start(bf16[2,64,1,4096]{3,1,2,0:T(8,128)(2,1)S(1)} %copy-done), channel_id=1, source_target_pairs={{1,0},{0,1},{3,2},{2,3},{5,4},{4,5},{7,6},{6,7},{9,8},{8,9},{11,10... | collective-permute-start | bytes 3145736 | tf_op jit(solution)/shard_map/ppermute | solution.py:18
  115.5 3.1 %copy-start.2 = (bf16[1,4,64,4096]{3,2,0,1:T(8,128)(2,1)S(1)}, bf16[1,4,64,4096]{3,2,0,1:T(8,128)(2,1)}, u32[]{:S(2)}) copy-start(bf16[1,4,64,4096]{3,2,0,1:T(8,128)(2,1)} %get-tuple-element.6) | copy-start | bytes 6291460
  118.7 2.8 %copy-start.4 = (bf16[2,256,1,4096]{3,1,2,0:T(8,128)(2,1)S(1)}, bf16[2,256,1,4096]{3,1,2,0:T(8,128)(2,1)}, u32[]{:S(2)}) copy-start(bf16[2,256,1,4096]{3,1,2,0:T(8,128)(2,1)} %all-gather.3.cloned.1.call-done) | copy-start | bytes 12582916
  121.5 1.6 %copy-start.1 = (bf16[1,4,64,4096]{3,2,0,1:T(8,128)(2,1)S(1)}, bf16[1,4,64,4096]{3,2,0,1:T(8,128)(2,1)}, u32[]{:S(2)}) copy-start(bf16[1,4,64,4096]{3,2,0,1:T(8,128)(2,1)} %get-tuple-element.7) | copy-start | bytes 6291460
  125.3 13.3 %copy-start.3 = (f32[1,4096]{1,0:T(1,128)S(1)}, f32[1,4096]{1,0:T(1,128)}, u32[]{:S(2)}) copy-start(f32[1,4096]{1,0:T(1,128)} %param.3) | copy-start | bytes 49156
  133.8 14.2 %all-to-all-start.1 = ((f32[128,2,256]{0,1,2:T(2,128)}), f32[128,2,256]{0,1,2:T(2,128)S(1)}, u32[]{:S(2)}, u32[]{:S(2)}) async-start(f32[128,2,256]{0,1,2:T(2,128)} %copy.7), calls=%async_computation.2 | async-start | bytes 524288 | tf_op jit(solution)/shard_map/all_to_all | solution.py:65
Sparse Core Ops, SparseCore 0:
  20.0 54.0 all-gather.2
  124.8 7.0 reduce-scatter.1
